TPU v7x, 128 devices: a whole 4x4x4 slice. The times are simulated.
128 devices in a mesh: band: 8 (over y, x_lo), chan: 16 (over x_hi, z, core).
Axes of the slice: x: 4 (x_hi: 2, x_lo: 2; x = x_hi * 2 + x_lo), y: 4, z: 4, core: 2. Of those that a mesh axis runs over, the one named last changes fastest.
Arguments:
- coeffs: bfloat16 [2, 8, 1024, 8192], P(None, None, 'chan', 'band'), may hold values from -1100 to 1100, as said below
Outputs:
- coherence: float32 [1024, 1024], P('chan', 'band')
Inputs may be any that keep to these rules, and one draw needn't show every extreme that they name: `coeffs`: finite real and imaginary parts.
All inputs are finite; a program needn't handle non-finite values.
Results may differ from a plain program's by a relative error of at most 0.0003.
Values may be sent and summed in bfloat16 or wider, within the bound.
A program may use at most 192 MiB of HBM per device.

v0:
```python
import jax
import jax.numpy as jnp
from jax import lax
from jax.sharding import PartitionSpec as P

K = 8
W = 16
epsilon = 1e-06


def in_blocks(shard, dim, length):
    dims = shard.shape
    tiles = shard.reshape(*dims[:dim], length, dims[dim] // length, *dims[dim + 1 :])
    return jnp.moveaxis(tiles, dim, 0)


def sent_and_summed(shard, axis, dim):
    length = lax.axis_size(axis)
    tiles = lax.all_to_all(in_blocks(shard, dim, length), axis, 0, 0, tiled=True)
    return jnp.sum(tiles, axis=0)


def body(coeffs):
    num_bands = coeffs.shape[3] // W
    own_width = coeffs.shape[2]
    cycle_size = lax.axis_size("chan")
    own_index = lax.axis_index("chan")
    full_width = own_width * cycle_size
    group_count = lax.axis_size("band")
    scale = jnp.float32(W * K / (num_bands * group_count))
    local_rows = coeffs.reshape(2, K, own_width, num_bands, W)
    paired = jnp.stack((local_rows[1], -local_rows[0]), axis=0)
    left_side = jnp.concatenate((local_rows, paired), axis=2)
    wide_rows = local_rows.astype(jnp.float32)
    own_power = jnp.sum(wide_rows * wide_rows, axis=(0, 1, 4)).T + epsilon
    piece = lax.all_gather(coeffs, "chan", axis=2, tiled=True)
    count = piece.shape[2]
    right_side = piece.reshape(2, K, count, num_bands, W)
    product = jnp.einsum(
        "pkinw,pkjnw->nij", left_side, right_side, preferred_element_type=jnp.float32
    )
    real_part = product[:, :own_width, :]
    imag_part = product[:, own_width:, :]
    wide_piece = right_side.astype(jnp.float32)
    piece_power = jnp.sum(wide_piece * wide_piece, axis=(0, 1, 4)).T + epsilon
    coh_band = (real_part * real_part + imag_part * imag_part) / (
        own_power[:, :, None] * piece_power[:, None, :]
    )
    partial_value = jnp.sum(coh_band, axis=0)
    row_global = lax.broadcasted_iota(jnp.int32, (own_width, full_width), 0) + own_index * own_width
    col_global = lax.broadcasted_iota(jnp.int32, (own_width, full_width), 1)
    partial_value = jnp.where(row_global == col_global, jnp.float32(0.0), partial_value)
    result = sent_and_summed(partial_value, "band", 1)
    return result * scale


def solution(mesh):
    return jax.shard_map(
        body,
        mesh=mesh,
        in_specs=(P(None, None, "chan", "band"),),
        out_specs=P("chan", "band"),
        check_vma=False,
    )
```

profile of v0, /device:TPU:0, one launch (start us, length us, event | category | flops | bytes accessed | tf_op | source)
XLA Modules:
  0.0 327.6 jit_solution(6133088543758207707)
XLA Ops:
  6.5 0.0 copy-start
  6.5 0.0 all-gather.2.cloned.1.call-start
  6.5 4.2 %copy.37 = bf16[2,8,64,1024]{3,1,0,2:T(8,128)(2,1)} copy(bf16[2,8,64,1024]{3,2,1,0:T(8,128)(2,1)} %param.1) | data formatting | bytes 4194304 | tf_op args[0]
  10.7 0.0 all-gather.2.cloned.1.call-update
  10.8 0.0 copy-done
  10.8 3.2 copy.31
  14.0 0.4 multiply_reduce_fusion.1
  14.4 0.2 copy.40
  14.6 0.1 bitcast_reduce_fusion.1
  14.7 4.0 %fusion.14 = (bf16[1,8,64,1024]{2,3,1,0:T(8,128)(2,1)S(1)}, bf16[1,8,64,1024]{2,3,1,0:T(8,128)(2,1)}) fusion(bf16[2,8,64,1024]{2,3,1,0:T(8,128)(2,1)} %copy.31), kind=kLoop, calls=%fused_computation.25 | loop fusion | flops 524288 | bytes 4194304 | tf_op jit(solution)/shard_map/slice | solution.py:32
  18.7 180.3 %all-gather.2.cloned.1.call-done = bf16[2,8,1024,1024]{3,1,0,2:T(8,128)(2,1)} async-done(((bf16[2,8,64,1024]{3,1,0,2:T(8,128)(2,1)}), bf16[2,8,1024,1024]{3,1,0,2:T(8,128)(2,1)}) %all-gather.2.cloned.1.call-update) | async-done | bytes 33554448 | tf_op jit(solution)/shard_map/all_gather | solution.py:36
  199.1 18.3 %multiply_reduce_fusion = f32[1024,1024]{1,0:T(8,128)} fusion(bf16[2,8,1024,1024]{3,1,0,2:T(8,128)(2,1)} %all-gather.2.cloned.1.call-done), kind=kLoop, calls=%fused_computation | loop fusion | flops 49283072 | bytes 37748736 | tf_op jit(solution)/shard_map/reduce_sum | solution.py:45
  217.3 5.3 %copy.41 = f32[1024,1024]{0,1:T(8,128)} copy(f32[1024,1024]{1,0:T(8,128)} %multiply_reduce_fusion) | data formatting | bytes 8388608 | tf_op jit(solution)/shard_map/reduce_sum | solution.py:45
  222.7 3.1 bitcast_reduce_fusion
  225.8 45.1 %copy.38 = bf16[2,8,1024,1024]{2,3,1,0:T(8,128)(2,1)} copy(bf16[2,8,1024,1024]{3,1,0,2:T(8,128)(2,1)} %all-gather.2.cloned.1.call-done) | data formatting | bytes 67108864 | tf_op jit(solution)/shard_map/all_gather | solution.py:36
  271.0 25.2 %fusion.5 = f32[64,128,1024]{2,1,0:T(8,128)} fusion(bf16[2,8,1024,64,16]{2,4,3,1,0:T(8,128)(2,1)} %bitcast.24, bf16[1,8,64,64,16]{2,4,0,3,1:T(8,128)(2,1)} %bitcast.27, bf16[1,8,64,64,16]{2,4,0,3,1:T(8,128)(2,1)S(1)} %bitcast.26, bf16[2,8,64,64,16]{2,4,3,1,0:T(8,128)(2,1)} %bitcast.25), kind=kOutput, calls=%fused_computation.8 | convolution fusion | flops 4307550208 | bytes 71303168 | tf_op jit(solution)/shard_map/pkinw,pkjnw->nij/dot_general | solution.py:39
  296.2 11.9 %fusion.4 = f32[64,1024]{1,0:T(8,128)S(1)} fusion(f32[64,128,1024]{2,1,0:T(8,128)} %fusion.5, f32[64,1024]{1,0:T(8,128)S(1)} %add_bitcast_fusion, f32[64,64]{1,0:T(8,128)S(1)} %add_bitcast_fusion.1), kind=kLoop, calls=%fused_computation.7 | loop fusion | flops 25100288 | bytes 34095104 | tf_op jit(solution)/shard_map/reduce_sum | solution.py:49
  308.1 0.1 bitcast_select_fusion
  308.3 0.1 copy.42
  308.3 11.8 %all_to_all.5 = f32[8,64,128]{2,1,0:T(8,128)S(1)} all-to-all(f32[8,64,128]{2,1,0:T(8,128)S(1)} %copy.42), channel_id=1, replica_groups=mesh['band'=8,'chan'=16] {'band'}, dimensions={0} | all-to-all | bytes 524288 | tf_op jit(solution)/shard_map/all_to_all | solution.py:19
  320.1 0.6 broadcast_multiply_fusion
  (6 shorter events, 0.1 us)
Async XLA Ops:
  6.5 4.2 %copy-start = (bf16[2,8,64,1024]{3,2,1,0:T(8,128)(2,1)S(1)}, bf16[2,8,64,1024]{3,2,1,0:T(8,128)(2,1)}, u32[]{:S(2)}) copy-start(bf16[2,8,64,1024]{3,2,1,0:T(8,128)(2,1)} %param.1) | copy-start | bytes 6291460
  6.5 192.5 %all-gather.2.cloned.1.call-start = ((), (), s32[]{:S(2)}) async-start(), calls=%async_computation.1 | async-start | bytes 35651584 | tf_op jit(solution)/shard_map/all_gather | solution.py:36
Sparse Core Ops, SparseCore 0:
  10.9 188.1 all-gather.1
where the time goes:
time: 329 us; the launch traced here: 328 us
  waiting for transfers between devices  180 us (55%)
  local copies, waits for them, and re-layouts  58.2 us (18%)
  other arithmetic  38.6 us (12%)
  matrix products  25.2 us (8%)
  between operations  13.5 us (4%)
  blocking collectives  11.8 us (4%)
    all_gather x1, waiting for transfers between devices, body(): piece = lax.all_gather(coeffs, 'chan', axis=2, tiled=True)  180 us
    all_gather x1, local copies, waits for them, and re-layouts, body(): piece = lax.all_gather(coeffs, 'chan', axis=2, tiled=True)  45.1 us
    dot_general x1, matrix products, body(): jnp.einsum('pkinw,pkjnw->nij', left_side, right_side, preferred_element_t...  25.2 us
    reduce_sum x2, other arithmetic, body(): piece_power = jnp.sum(wide_piece * wide_piece, axis=(0, 1, 4)).T + epsilon  21.4 us
    reduce_sum x1, other arithmetic, body(): partial_value = jnp.sum(coh_band, axis=0)  11.9 us
    all_to_all x1, blocking collectives, sent_and_summed(): lax.all_to_all(in_blocks(shard, dim, length), axis, 0, 0, tiled=True)  11.8 us
    unnamed x5, local copies, waits for them, and re-layouts  7.43 us
  transfers between devices with their start and end apart: 1, of which 1 were waited for; matrix products, arithmetic and copies ran while one was open for 2% of the time, Pallas kernels for 0%

commit v1 on v0

--- a/solution.py
+++ b/solution.py
@@ -33,7 +33,7 @@
     left_side = jnp.concatenate((local_rows, paired), axis=2)
     wide_rows = local_rows.astype(jnp.float32)
     own_power = jnp.sum(wide_rows * wide_rows, axis=(0, 1, 4)).T + epsilon
-    piece = lax.all_gather(coeffs, "chan", axis=2, tiled=True)
+    piece = jnp.concatenate(lax.all_gather(coeffs, "chan"), axis=2)
     count = piece.shape[2]
     right_side = piece.reshape(2, K, count, num_bands, W)
     product = jnp.einsum(

time: 329 us -> 459 us (1.40)
  local copies, waits for them, and re-layouts: 58.2 us -> 177 us
  other arithmetic: 38.6 us -> 45 us
    another operation x0 -> x1, local copies, waits for them, and re-layouts: none -> 86.9 us  [body(): right_side = piece.reshape(2, K, count, num_bands, W)]
    all_gather x1, local copies, waits for them, and re-layouts: 45.1 us -> 77.6 us  [body(): piece = jnp.concatenate(lax.all_gather(coeffs, 'chan'), axis=2)]
    reduce_sum x2, other arithmetic: 21.4 us -> 27.8 us  [body(): piece_power = jnp.sum(wide_piece * wide_piece, axis=(0, 1, 4)).T + epsilon]
where the time goes in v1:
time: 459 us; the launch traced here: 455 us
  waiting for transfers between devices  182 us (40%)
  local copies, waits for them, and re-layouts  177 us (39%)
  other arithmetic  45 us (10%)
  matrix products  25.2 us (5%)
  between operations  13.5 us (3%)
  blocking collectives  11.8 us (3%)
    all_gather x1, waiting for transfers between devices, body(): piece = jnp.concatenate(lax.all_gather(coeffs, 'chan'), axis=2)  181 us
    another operation x1, local copies, waits for them, and re-layouts, body(): right_side = piece.reshape(2, K, count, num_bands, W)  86.9 us
    all_gather x1, local copies, waits for them, and re-layouts, body(): piece = jnp.concatenate(lax.all_gather(coeffs, 'chan'), axis=2)  77.6 us
    reduce_sum x2, other arithmetic, body(): piece_power = jnp.sum(wide_piece * wide_piece, axis=(0, 1, 4)).T + epsilon  27.8 us
    dot_general x1, matrix products, body(): jnp.einsum('pkinw,pkjnw->nij', left_side, right_side, preferred_element_t...  25.2 us
    reduce_sum x1, other arithmetic, body(): partial_value = jnp.sum(coh_band, axis=0)  11.9 us
    all_to_all x1, blocking collectives, sent_and_summed(): lax.all_to_all(in_blocks(shard, dim, length), axis, 0, 0, tiled=True)  11.8 us
  transfers between devices with their start and end apart: 1, of which 1 were waited for; matrix products, arithmetic and copies ran while one was open for 2% of the time, Pallas kernels for 0%

profile of v1, /device:TPU:0, one launch (start us, length us, event | category | flops | bytes accessed | tf_op | source)
XLA Modules:
  0.0 454.5 jit_solution(1168359111608429131)
XLA Ops:
  6.5 0.0 copy-start
  6.5 0.0 all-gather.3.cloned.1.call-start
  6.5 0.7 all-gather.3.cloned.1.call-update
  7.3 4.8 %copy.19 = bf16[2,8,64,1024]{2,3,1,0:T(8,128)(2,1)} copy(bf16[2,8,64,1024]{3,2,1,0:T(8,128)(2,1)} %param.1) | data formatting | bytes 4194304 | tf_op args[0]
  12.0 0.0 copy-done
  12.0 0.4 multiply_reduce_fusion.1
  12.5 0.2 copy.27
  12.7 0.1 bitcast_reduce_fusion
  12.8 3.9 fusion.14
  16.7 181.2 %all-gather.3.cloned.1.call-done = bf16[32,8,64,1024]{3,2,1,0:T(8,128)(2,1)} async-done(((bf16[2,8,64,1024]{3,2,1,0:T(8,128)(2,1)}), bf16[32,8,64,1024]{3,2,1,0:T(8,128)(2,1)}) %all-gather.3.cloned.1.call-update) | async-done | bytes 33554448 | tf_op jit(solution)/shard_map/all_gather | solution.py:36
  198.0 77.6 %copy.25 = bf16[16,2,8,64,1024]{3,0,4,2,1:T(8,128)(2,1)} copy(bf16[16,2,8,64,1024]{4,3,2,1,0:T(8,128)(2,1)} %bitcast.31) | data formatting | bytes 67108864 | tf_op jit(solution)/shard_map/all_gather | solution.py:36
  275.6 24.7 %multiply_reduce_fusion = f32[16,64,1024]{1,0,2:T(8,128)} fusion(bf16[16,2,8,64,1024]{3,0,4,2,1:T(8,128)(2,1)} %copy.25), kind=kLoop, calls=%fused_computation | loop fusion | flops 49283072 | bytes 37748736 | tf_op jit(solution)/shard_map/reduce_sum | solution.py:45
  300.3 7.6 %reduce_sum.56 = f32[1024,64,16]{0,2,1:T(8,128)} reshape(f32[16,64,1024]{1,0,2:T(8,128)} %multiply_reduce_fusion) | data formatting | bytes 8388608 | tf_op jit(solution)/shard_map/reduce_sum | solution.py:45
  307.9 3.1 reduce_sum.57
  311.0 86.9 %reshape_reshape.3 = bf16[2,8,1024,64,16]{2,4,3,1,0:T(8,128)(2,1)} reshape(bf16[2,8,16,64,1024]{3,2,4,1,0:T(8,128)(2,1)} %bitcast.6) | data formatting | bytes 67108864 | tf_op jit(solution)/shard_map/reshape;reshape | solution.py:38
  397.9 25.2 %fusion.5 = f32[64,128,1024]{2,1,0:T(8,128)} fusion(bf16[2,8,1024,64,16]{2,4,3,1,0:T(8,128)(2,1)} %reshape_reshape.3, bf16[1,8,64,64,16]{2,4,0,3,1:T(8,128)(2,1)} %bitcast.33, bf16[1,8,64,64,16]{2,4,0,3,1:T(8,128)(2,1)S(1)} %bitcast.32, bf16[2,8,64,64,16]{2,4,3,1,0:T(8,128)(2,1)} %bitcast.30), kind=kOutput, calls=%fused_computation.8 | convolution fusion | flops 4307550208 | bytes 71303168 | tf_op jit(solution)/shard_map/pkinw,pkjnw->nij/dot_general | solution.py:39
  423.1 11.9 %fusion.4 = f32[64,1024]{1,0:T(8,128)S(1)} fusion(f32[64,128,1024]{2,1,0:T(8,128)} %fusion.5, f32[64,1024]{1,0:T(8,128)S(1)} %add_bitcast_fusion, f32[64,64]{1,0:T(8,128)S(1)} %add_bitcast_fusion.1), kind=kLoop, calls=%fused_computation.7 | loop fusion | flops 25100288 | bytes 34095104 | tf_op jit(solution)/shard_map/reduce_sum | solution.py:49
  435.1 0.1 bitcast_select_fusion
  435.2 0.1 copy.28
  435.3 11.8 %all_to_all.5 = f32[8,64,128]{2,1,0:T(8,128)S(1)} all-to-all(f32[8,64,128]{2,1,0:T(8,128)S(1)} %copy.28), channel_id=1, replica_groups=mesh['band'=8,'chan'=16] {'band'}, dimensions={0} | all-to-all | bytes 524288 | tf_op jit(solution)/shard_map/all_to_all | solution.py:19
  447.1 0.6 broadcast_multiply_fusion
  (6 shorter events, 0.1 us)
Async XLA Ops:
  6.5 5.5 %copy-start = (bf16[2,8,64,1024]{3,2,1,0:T(8,128)(2,1)S(1)}, bf16[2,8,64,1024]{3,2,1,0:T(8,128)(2,1)}, u32[]{:S(2)}) copy-start(bf16[2,8,64,1024]{3,2,1,0:T(8,128)(2,1)} %param.1) | copy-start | bytes 6291460
  6.5 191.4 %all-gather.3.cloned.1.call-start = ((), (), s32[]{:S(2)}) async-start(), calls=%async_computation.1 | async-start | bytes 35651584 | tf_op jit(solution)/shard_map/all_gather | solution.py:36
Sparse Core Ops, SparseCore 0:
  9.8 188.1 all-gather.2
